TPU v7x, 32 devices: a whole 2x2x4 slice. The times are simulated.
32 devices in a mesh: node: 8 (over y, x, core), stripe: 4 (over z).
Axes of the slice: x: 2, y: 2, z: 4, core: 2. Of those that a mesh axis runs over, the one named last changes fastest.
Arguments:
- groups: bfloat16 [4, 16, 256, 8, 512], P('stripe', 'node'), may hold values from -21 to 21
- gamma: float32 [8, 8], replicated, may hold values from -2 to 2
- coeffs: float32 [4, 12, 8, 8], replicated, may hold values from -0.625 to 0.625
Outputs:
- syndrome: float32 [256, 4, 4, 8, 512], P('node', 'stripe')
- scores: float32 [256, 4, 4], P('node', 'stripe')
All inputs are finite; a program needn't handle non-finite values.
Results may differ from a plain program's by a relative error of at most 0.0003.
Values may be sent and summed in bfloat16 or wider, within the bound.
No kernel may reach another device: no remote copies, remote signals or barrier semaphores. Data moves between devices by JAX's collectives and lax.ppermute only.
A program may use at most 64 MiB of HBM per device.

v0:
```python
import jax
import jax.numpy as jnp
from jax import lax
from jax.sharding import PartitionSpec as P

LAYERS = 256
PLANES = 8
PARITY = 4
DATA_NODES = 12
VIRTUAL = 2
precise = lax.Precision.HIGHEST
epsilon = 1e-06


def for_sending(x):
    return jax.tree.map(lambda a: a.astype(jnp.bfloat16) if a.dtype == jnp.float32 else a, x)


def from_behind(block, axis, distance):
    devices = range(lax.axis_size(axis))
    route = [((i - distance) % len(devices), i) for i in devices]
    return lax.ppermute(block, axis, route)


def mix_planes(matrix, values):
    return jnp.einsum("pq,...qb->...pb", matrix, values, precision=precise)


def inverse_factor(gamma):
    order_count = gamma.shape[0]
    identity = jnp.eye(order_count, dtype=jnp.float32)
    mixed = identity + jnp.dot(gamma.T, gamma, precision=precise)
    factor = jnp.linalg.cholesky(mixed)
    solved_rows = []
    for row_at in range(order_count):
        running = identity[row_at]
        for earlier in range(row_at):
            running = running - factor[row_at, earlier] * solved_rows[earlier]
        solved_rows.append(running / factor[row_at, row_at])
    solved = jnp.stack(solved_rows)
    return jnp.dot(solved.T, solved, precision=precise)


def to_front(values, digit_axis):

    def to_mover(position):
        return lambda operand: jnp.moveaxis(operand, 4 - position, 1)

    return lax.switch(digit_axis, [to_mover(position) for position in range(4)], values)


def from_front(values, digit_axis):

    def from_mover(position):
        return lambda operand: jnp.moveaxis(operand, 1, 4 - position)

    return lax.switch(digit_axis, [from_mover(position) for position in range(4)], values)


def local(groups, gamma, coeffs):
    stripes_here = groups.shape[0]
    nodes_here = groups.shape[1]
    byte_count = groups.shape[4]
    device = lax.axis_index("node")
    first_node = device * nodes_here
    column = first_node // 4
    inverse = inverse_factor(gamma)
    node_ids = first_node + jnp.arange(nodes_here)
    keep_mask = ((node_ids < DATA_NODES - VIRTUAL) | (node_ids >= DATA_NODES)).astype(jnp.bfloat16)
    stored = groups * keep_mask[None, :, None, None, None]
    fronts = []
    for local_node in range(nodes_here):
        row_index = (first_node + local_node) % 4
        layer_grid = stored[:, local_node].reshape(stripes_here, 4, 4, 4, 4, PLANES, byte_count)
        fronts.append(
            to_front(layer_grid, row_index).reshape(
                stripes_here, 4, LAYERS // 4, PLANES, byte_count
            )
        )
    fronted = jnp.stack(fronts, axis=1)
    step_nodes = 4 // nodes_here
    received = []
    for offset in range(1, 4):
        partner_piece = from_behind(
            for_sending(
                lax.dynamic_index_in_dim(fronted, (column + offset) % 4, axis=2, keepdims=False)
            ),
            "node",
            offset * step_nodes,
        )
        received.append(((column - offset) % 4, partner_piece))
    own_front = fronted.astype(jnp.float32)
    result = own_front
    for slot_index, partner_piece in received:
        own_rows = lax.dynamic_index_in_dim(own_front, slot_index, axis=2, keepdims=False)
        theirs = partner_piece.astype(jnp.float32)
        own_lower = column < slot_index
        lower_rows = jnp.where(own_lower, own_rows, theirs)
        upper_rows = jnp.where(own_lower, theirs, own_rows)
        upper_part = mix_planes(inverse, upper_rows + mix_planes(gamma.T, lower_rows))
        values = jnp.where(own_lower, lower_rows - mix_planes(gamma, upper_part), upper_part)
        result = lax.dynamic_update_index_in_dim(result, values, slot_index, axis=2)
    backs = []
    for local_node in range(nodes_here):
        row_index = (first_node + local_node) % 4
        layer_grid = result[:, local_node].reshape(stripes_here, 4, 4, 4, 4, PLANES, byte_count)
        backs.append(
            from_front(layer_grid, row_index).reshape(stripes_here, LAYERS, PLANES, byte_count)
        )
    uncoupled = jnp.stack(backs, axis=1)
    identity = jnp.eye(PLANES, dtype=jnp.float32)
    blocks = jnp.eye(PARITY, dtype=jnp.float32)[:, :, None, None] * identity[None, None]
    weights_all = jnp.concatenate([-coeffs, blocks], axis=1)
    syndrome = jnp.einsum(
        "ijpq,sjlqb->lsipb",
        weights_all,
        lax.all_to_all(uncoupled, "node", split_axis=2, concat_axis=1, tiled=True),
        precision=precise,
    )
    energy = jnp.mean(syndrome * syndrome, axis=(3, 4))
    pool_sum = lax.psum(jnp.sum(energy, axis=1), "stripe")
    stripe_total = stripes_here * lax.axis_size("stripe")
    scores = energy / (pool_sum[:, None, :] / stripe_total + epsilon)
    return (syndrome, scores)


def solution(mesh):
    return jax.shard_map(
        local,
        mesh=mesh,
        in_specs=(P("stripe", "node", None, None, None), P(), P()),
        out_specs=(P("node", "stripe", None, None, None), P("node", "stripe", None)),
        check_vma=False,
    )
```

profile of v0, /device:TPU:0, one launch (start us, length us, event | category | flops | bytes accessed | tf_op | source)
XLA Modules:
  0.0 257.2 jit_solution(47889790480864739)
XLA Ops:
  0.8 2.5 broadcast_multiply_fusion
  7.4 3.1 %conditional.4 = (bf16[1,1,4,64,8,512]{5,4,2,3,1,0:T(8,128)(2,1)}) conditional(s32[]{:T(128)} %clamp.8, bf16[1,2,256,8,512]{4,3,2,1,0:T(8,128)(2,1)} %copy-done.3, bf16[1,2,256,8,512]{4,3,2,1,0:T(8,128)(2,1)} %copy-done.3, bf16[1,2,256,8,512]{4,3,2,1,0:T(8,128)(2,1)} %copy-done.3, ...), branch_computations={%region_0.1_spmd, %region_1.2_spmd, %region_2.3_spmd, %region_3.4_... | conditional | bytes 14680096 | solution.py:49
  7.4 3.1 %slice.130 = bf16[1,1,256,8,512]{4,3,2,1,0:T(8,128)(2,1)} slice(bf16[1,2,256,8,512]{4,3,2,1,0:T(8,128)(2,1)} %param), slice={[0:1], [0:1], [0:256], [0:8], [0:512]} | slice | bytes 4194304 | tf_op jit(solution)/shard_map/slice | solution.py:74
  10.4 6.8 %fusion.75 = (bf16[1,2,4,64,8,512]{5,4,3,2,1,0:T(8,128)(2,1)}, f32[1,2,4,64,8,512]{5,4,3,2,1,0:T(8,128)}) fusion(bf16[1,1,4,64,8,512]{5,4,2,3,1,0:T(8,128)(2,1)} %copy-done.4, bf16[1,1,4,64,8,512]{5,4,2,3,1,0:T(8,128)(2,1)} %get-tuple-element.139), kind=kLoop, calls=%fused_computation.104 | loop fusion | flops 4194304 | bytes 16777216 | tf_op jit(solution)/shard_map/stack | solution.py:80
  17.2 3.6 %dynamic-slice_bitcast_fusion = (bf16[1,2,64,8,512]{4,3,2,1,0:T(8,128)(2,1)}, bf16[1,2,64,8,512]{4,3,2,1,0:T(8,128)(2,1)}, bf16[1,2,64,8,512]{4,3,2,1,0:T(8,128)(2,1)}) fusion(bf16[1,2,4,64,8,512]{5,4,3,2,1,0:T(8,128)(2,1)} %get-tuple-element.99, s32[]{:T(128)S(6)} %select_n.139, s32[]{:T(128)S(6)} %select_n.131, s32[]{:T(128)S(6)} %select_n.122), kind=kLoop, calls=%fused_computation.54 | loop fusion | bytes 6291468 | tf_op jit(solution)/shard_map/jit(dynamic_index_in_dim)/squeeze | solution.py:86
  20.8 3.0 %collective-permute-start = (bf16[1,2,64,8,512]{4,3,2,1,0:T(8,128)(2,1)}, bf16[1,2,64,8,512]{4,3,2,1,0:T(8,128)(2,1)S(1)}, u32[]{:S(2)}, u32[]{:S(2)}) collective-permute-start(bf16[1,2,64,8,512]{4,3,2,1,0:T(8,128)(2,1)} %get-tuple-element.98), channel_id=1, source_target_pairs={{24,0},{28,4},{0,8},{4,12},{8,16},{12,20},{16,24},{20,28},{25,1},{... | collective-permute-start | bytes 3145736 | tf_op jit(solution)/shard_map/ppermute | solution.py:22
  28.3 7.6 %copy.162 = f32[1,2,4,64,8,512]{5,4,3,2,1,0:T(8,128)} copy(f32[1,2,4,64,8,512]{5,4,3,2,1,0:T(8,128)} %get-tuple-element.100) | data formatting | bytes 16777216
  38.5 22.5 %subtract_divide_fusion = (f32[1,8]{1,0:T(1,128)S(1)}, f32[1,8]{1,0:T(1,128)S(1)}, f32[1,8]{1,0:T(1,128)S(1)}, f32[1,8]{1,0:T(1,128)S(1)}, f32[1,8]{1,0:T(1,128)...) fusion(f32[8,8]{1,0:T(8,128)S(1)} %fusion.66, f32[]{:T(128)} %bitcast.83, f32[]{:T(128)} %bitcast.82, ...), kind=kLoop, calls=%fused_computation.94 | loop fusion | flops 512 | bytes 656 | tf_op jit(solution)/shard_map/div | solution.py:39
  67.5 3.2 %collective-permute-done.1 = bf16[1,2,64,8,512]{4,3,2,1,0:T(8,128)(2,1)S(1)} collective-permute-done((bf16[1,2,64,8,512]{4,3,2,1,0:T(8,128)(2,1)}, bf16[1,2,64,8,512]{4,3,2,1,0:T(8,128)(2,1)S(1)}, u32[]{:S(2)}, u32[]{:S(2)}) %collective-permute-start.1) | collective-permute-done | bytes 1048608 | tf_op jit(solution)/shard_map/ppermute | solution.py:22
  75.1 4.0 %bitcast_dynamic-update-slice_fusion.2 = f32[1,2,4,64,8,512]{5,4,3,2,1,0:T(8,128)} fusion(f32[1,2,4,64,8,512]{5,4,3,2,1,0:T(8,128)} %copy.162, s32[]{:T(128)S(6)} %select_n.120, f32[1,2,64,8,512]{4,3,2,1,0:T(8,128)S(1)} %convert_select_fusion.5, f32[2,64,512,8]{2,3,1,0:T(8,128)S(1)} %fusion.4, pred[]{:T(512)S(6)} %lt.82, f32[8,8]{1,0:T(8,128)S(1)} %copy-done), kind=kOutput, calls=%fused_computation.32 | convolution fusion | flops 51380224 | bytes 8392709 | tf_op jit(solution)/shard_map/pq,...qb->...pb/dot_general | solution.py:26
  83.5 3.9 %bitcast_dynamic-update-slice_fusion.1 = f32[1,2,4,64,8,512]{5,4,3,2,1,0:T(8,128)} fusion(f32[1,2,4,64,8,512]{5,4,3,2,1,0:T(8,128)} %bitcast_dynamic-update-slice_fusion.2, s32[]{:T(128)S(6)} %select_n.129, f32[2,64,512,8]{2,3,1,0:T(8,128)S(1)} %fusion.8, bf16[1,2,64,8,512]{4,3,2,1,0:T(8,128)(2,1)S(1)} %collective-permute-done.1, ...), kind=kOutput, calls=%fused_computation.26 | convolution fusion | flops 52428800 | bytes 9441285 | tf_op jit(solution)/shard_map/pq,...qb->...pb/dot_general | solution.py:26
  87.4 3.9 %bitcast_dynamic-update-slice_fusion = f32[1,2,4,64,8,512]{5,4,3,2,1,0:T(8,128)} fusion(f32[1,2,4,64,8,512]{5,4,3,2,1,0:T(8,128)} %bitcast_dynamic-update-slice_fusion.1, s32[]{:T(128)S(6)} %select_n.137, f32[2,64,512,8]{2,3,1,0:T(8,128)S(1)} %fusion.12, bf16[1,2,64,8,512]{4,3,2,1,0:T(8,128)(2,1)S(1)} %collective-permute-done.2, ...), kind=kOutput, calls=%fused_computation.20 | convolution fusion | flops 52428800 | bytes 9441285 | tf_op jit(solution)/shard_map/pq,...qb->...pb/dot_general | solution.py:26
  91.3 5.3 %conditional.7 = (f32[1,1,256,8,512]{4,3,2,1,0:T(8,128)}) conditional(s32[]{:T(128)} %clamp.9, f32[1,2,4,64,8,512]{5,4,3,2,1,0:T(8,128)} %bitcast_dynamic-update-slice_fusion, f32[1,2,4,64,8,512]{5,4,3,2,1,0:T(8,128)} %bitcast_dynamic-update-slice_fusion, ...), branch_computations={%region_14.15_spmd, %region_15.16_spmd, %region_16.17_spmd, %regio... | conditional | bytes 16777224 | solution.py:57
  91.3 2.6 %slice.143 = f32[1,1,4,64,8,512]{5,4,3,2,1,0:T(8,128)S(1)} slice(f32[1,2,4,64,8,512]{5,4,3,2,1,0:T(8,128)} %param.13), slice={[0:1], [1:2], [0:4], [0:64], [0:8], [0:512]} | slice | bytes 8388608 | tf_op jit(solution)/shard_map/slice | solution.py:106
  96.6 5.2 %conditional.6 = (f32[1,1,256,8,512]{4,3,2,1,0:T(8,128)}) conditional(s32[]{:T(128)} %clamp.8, f32[1,2,4,64,8,512]{5,4,3,2,1,0:T(8,128)} %bitcast_dynamic-update-slice_fusion, f32[1,2,4,64,8,512]{5,4,3,2,1,0:T(8,128)} %bitcast_dynamic-update-slice_fusion, ...), branch_computations={%region_10.11_spmd, %region_11.12_spmd, %region_12.13_spmd, %regio... | conditional | bytes 16777224 | solution.py:57
  96.6 2.6 %slice.138 = f32[1,1,4,64,8,512]{5,4,3,2,1,0:T(8,128)S(1)} slice(f32[1,2,4,64,8,512]{5,4,3,2,1,0:T(8,128)} %param.8), slice={[0:1], [0:1], [0:4], [0:64], [0:8], [0:512]} | slice | bytes 8388608 | tf_op jit(solution)/shard_map/slice | solution.py:106
  99.2 2.6 %copy.116 = f32[1,4,4,4,4,8,512]{6,5,1,4,3,2,0:T(8,128)} copy(f32[1,4,4,4,4,8,512]{6,5,4,3,2,1,0:T(8,128)S(1)} %bitcast.307) | data formatting | bytes 8388608 | tf_op jit(solution)/shard_map/reshape;squeeze | solution.py:106
  101.8 7.9 %pad_maximum_fusion = f32[1,2,256,8,512]{4,3,1,0,2:T(8,128)} fusion(f32[1,1,256,8,512]{4,3,1,0,2:T(8,128)} %bitcast.314, f32[1,1,256,8,512]{4,3,1,0,2:T(8,128)} %bitcast.319), kind=kLoop, calls=%fused_computation | loop fusion | flops 2097152 | bytes 16777216 | tf_op jit(solution)/shard_map/stack | solution.py:110
  109.8 5.2 %all-to-all-start = ((f32[1,2,256,8,512]{4,3,1,0,2:T(8,128)}), f32[1,2,256,8,512]{4,3,1,0,2:T(8,128)}, u32[]{:S(2)}, u32[]{:S(2)}) async-start(f32[1,2,256,8,512]{4,3,1,0,2:T(8,128)} %pad_maximum_fusion), calls=%async_computation | async-start | bytes 16777216 | tf_op jit(solution)/shard_map/all_to_all | solution.py:117
  115.1 93.8 %all-to-all-done = f32[1,2,256,8,512]{4,3,1,0,2:T(8,128)} async-done(((f32[1,2,256,8,512]{4,3,1,0,2:T(8,128)}), f32[1,2,256,8,512]{4,3,1,0,2:T(8,128)}, u32[]{:S(2)}, u32[]{:S(2)}) %all-to-all-start) | async-done | bytes 8388640 | tf_op jit(solution)/shard_map/all_to_all | solution.py:117
  209.0 15.4 %copy.153 = f32[1,2,8,32,8,512]{5,1,2,4,3,0:T(2,128)} copy(f32[1,2,8,32,8,512]{5,4,1,3,2,0:T(8,128)} %bitcast.127) | data formatting | bytes 16777216 | tf_op jit(solution)/shard_map/all_to_all | solution.py:117
  224.4 10.9 %reshape.144 = f32[16,32,8,512,1]{3,0,2,1,4:T(8,128)} reshape(f32[1,8,2,32,8,512]{5,2,1,4,3,0:T(2,128)} %bitcast.303) | data formatting | bytes 16777216 | tf_op jit(solution)/shard_map/reshape.26
  235.2 8.9 %fusion.26 = (f32[32,4]{1,0:T(8,128)S(1)}, f32[32,512,4,8,1]{1,3,4,2,0:T(8,128)}) fusion(f32[4,4,8,8]{1,2,3,0:T(8,128)S(1)} %broadcast_multiply_fusion.1, f32[4,12,8,8]{1,2,3,0:T(8,128)S(1)} %copy_negate_fusion, f32[16,32,8,512,1]{3,0,2,1,4:T(8,128)} %reshape.144), kind=kOutput, calls=%fused_computation.39 | convolution fusion | flops 806358912 | bytes 10502656 | tf_op jit(solution)/shard_map/ijpq,sjlqb->lsipb/dot_general | solution.py:114
  244.2 12.1 %psum.7 = f32[32,4]{0,1:T(4,128)S(1)} all-reduce(f32[32,4]{0,1:T(4,128)S(1)} %broadcast_multiply_fusion.2), channel_id=1, replica_groups=mesh['node'=8,'stripe'=4] {'stripe'}, use_global_device_ids=true, to_apply=%region_19.20 | all-reduce | flops 128 | bytes 1024 | tf_op jit(solution)/shard_map/psum | solution.py:121
  (48 shorter events, 30.3 us)
Async XLA Ops:
  0.6 26.5 %copy-start = (f32[8,8]{1,0:T(8,128)S(1)}, f32[8,8]{1,0:T(8,128)}, u32[]{:S(2)}) copy-start(f32[8,8]{1,0:T(8,128)} %param.20) | copy-start | bytes 772
  3.3 2.0 copy-start.3
  6.0 1.3 copy-start.4
  20.8 40.4 %collective-permute-start = (bf16[1,2,64,8,512]{4,3,2,1,0:T(8,128)(2,1)}, bf16[1,2,64,8,512]{4,3,2,1,0:T(8,128)(2,1)S(1)}, u32[]{:S(2)}, u32[]{:S(2)}) collective-permute-start(bf16[1,2,64,8,512]{4,3,2,1,0:T(8,128)(2,1)} %get-tuple-element.98), channel_id=1, source_target_pairs={{24,0},{28,4},{0,8},{4,12},{8,16},{12,20},{16,24},{20,28},{25,1},{... | collective-permute-start | bytes 3145736 | tf_op jit(solution)/shard_map/ppermute | solution.py:22
  23.8 47.0 %collective-permute-start.1 = (bf16[1,2,64,8,512]{4,3,2,1,0:T(8,128)(2,1)}, bf16[1,2,64,8,512]{4,3,2,1,0:T(8,128)(2,1)S(1)}, u32[]{:S(2)}, u32[]{:S(2)}) collective-permute-start(bf16[1,2,64,8,512]{4,3,2,1,0:T(8,128)(2,1)} %get-tuple-element.97), channel_id=1, source_target_pairs={{16,0},{20,4},{24,8},{28,12},{0,16},{4,20},{8,24},{12,28},{17,1},{... | collective-permute-start | bytes 3145736 | tf_op jit(solution)/shard_map/ppermute | solution.py:22
  25.3 53.8 %collective-permute-start.2 = (bf16[1,2,64,8,512]{4,3,2,1,0:T(8,128)(2,1)}, bf16[1,2,64,8,512]{4,3,2,1,0:T(8,128)(2,1)S(1)}, u32[]{:S(2)}, u32[]{:S(2)}) collective-permute-start(bf16[1,2,64,8,512]{4,3,2,1,0:T(8,128)(2,1)} %get-tuple-element.96), channel_id=1, source_target_pairs={{8,0},{12,4},{16,8},{20,12},{24,16},{28,20},{0,24},{4,28},{9,1},{1... | collective-permute-start | bytes 3145736 | tf_op jit(solution)/shard_map/ppermute | solution.py:22
  61.2 4.1 %copy-start.2 = (f32[1,2,4,64,8,512]{5,4,3,2,1,0:T(8,128)S(1)}, f32[1,2,4,64,8,512]{5,4,3,2,1,0:T(8,128)}, u32[]{:S(2)}) copy-start(f32[1,2,4,64,8,512]{5,4,3,2,1,0:T(8,128)} %get-tuple-element.100) | copy-start | bytes 25165828
  109.8 5.3 %copy-start.5 = (f32[4,12,8,8]{1,3,2,0:T(8,128)S(1)}, f32[4,12,8,8]{1,3,2,0:T(8,128)}, u32[]{:S(2)}) copy-start(f32[4,12,8,8]{1,3,2,0:T(8,128)} %param.21) | copy-start | bytes 36868
  109.8 99.2 %all-to-all-start = ((f32[1,2,256,8,512]{4,3,1,0,2:T(8,128)}), f32[1,2,256,8,512]{4,3,1,0,2:T(8,128)}, u32[]{:S(2)}, u32[]{:S(2)}) async-start(f32[1,2,256,8,512]{4,3,1,0,2:T(8,128)} %pad_maximum_fusion), calls=%async_computation | async-start | bytes 16777216 | tf_op jit(solution)/shard_map/all_to_all | solution.py:117
  235.2 21.7 %copy-start.1 = (f32[8,8]{1,0:T(8,128)S(1)}, f32[8,8]{1,0:T(8,128)}, u32[]{:S(2)}) copy-start(f32[8,8]{1,0:T(8,128)} %param.20) | copy-start | bytes 772
where the time goes:
time: 261 us; the launch traced here: 257 us
  waiting for transfers between devices  97 us (37%)
  local copies, waits for them, and re-layouts  56.5 us (22%)
  other arithmetic  44.5 us (17%)
  matrix products  34 us (13%)
  blocking collectives  12.1 us (5%)
  starting transfers between devices  11.5 us (4%)
    all_to_all x1, waiting for transfers between devices, local(): lax.all_to_all(uncoupled, 'node', split_axis=2, concat_axis=1, tiled=True)  93.8 us
    dot_general x9, matrix products, mix_planes(): return jnp.einsum('pq,...qb->...pb', matrix, values, precision=precise)  24.7 us
    div x1, other arithmetic, inverse_factor(): solved_rows.append(running / factor[row_at, row_at])  22.5 us
    all_to_all x1, local copies, waits for them, and re-layouts, local(): lax.all_to_all(uncoupled, 'node', split_axis=2, concat_axis=1, tiled=True)  15.4 us
    psum x1, blocking collectives, local(): pool_sum = lax.psum(jnp.sum(energy, axis=1), 'stripe')  12.1 us
    unnamed x13, local copies, waits for them, and re-layouts  11 us
    another operation x1, local copies, waits for them, and re-layouts  10.9 us
    dot_general x1, matrix products, local(): jnp.einsum('ijpq,sjlqb->lsipb', weights_all, lax.all_to_all(uncoupled, 'n...  8.93 us
  transfers between devices with their start and end apart: 4, of which 2 were waited for; matrix products, arithmetic and copies ran while one was open for 19% of the time, Pallas kernels for 0%

commit v1 on v0

--- a/solution.py
+++ b/solution.py
@@ -114,7 +114,12 @@
     syndrome = jnp.einsum(
         "ijpq,sjlqb->lsipb",
         weights_all,
-        lax.all_to_all(uncoupled, "node", split_axis=2, concat_axis=1, tiled=True),
+        jnp.concatenate(
+            lax.all_to_all(
+                jnp.stack(jnp.split(uncoupled, lax.axis_size("node"), axis=2)), "node", 0, 0
+            ),
+            axis=1,
+        ),
         precision=precise,
     )
     energy = jnp.mean(syndrome * syndrome, axis=(3, 4))

time: 261 us -> 241 us (0.923)
  local copies, waits for them, and re-layouts: 56.5 us -> 32.9 us
    all_to_all x1 -> x0, local copies, waits for them, and re-layouts: 15.4 us -> none  [local(): lax.all_to_all(uncoupled, 'node', split_axis=2, concat_axis=1, tiled=True)]
    another operation x1 -> x0, local copies, waits for them, and re-layouts: 10.9 us -> none
    unnamed x0 -> x8, other arithmetic: none -> 8.71 us
    another operation x1, other arithmetic: 7.92 us -> 1.12 us  [local(): jnp.stack(jnp.split(uncoupled, lax.axis_size('node'), axis=2))]
    dot_general x1, matrix products: 8.93 us -> 14.9 us  [local(): jnp.einsum('ijpq,sjlqb->lsipb', weights_all, jnp.concatenate(lax.all_to_a...]
    unnamed x13 -> x23, local copies, waits for them, and re-layouts: 11 us -> 15.8 us
    dot_general x9, matrix products: 24.7 us -> 20.3 us  [mix_planes(): return jnp.einsum('pq,...qb->...pb', matrix, values, precision=precise)]
  transfers between devices with their start and end apart: 4 -> 4, of which waited for: 2 -> 2; matrix products, arithmetic and copies ran while one was open for 19% -> 20% of each run, Pallas kernels for 0% -> 0%
where the time goes in v1:
time: 241 us; the launch traced here: 237 us
  waiting for transfers between devices  96.8 us (40%)
  other arithmetic  46.6 us (19%)
  matrix products  35.6 us (15%)
  local copies, waits for them, and re-layouts  32.9 us (14%)
  blocking collectives  12.1 us (5%)
  starting transfers between devices  11.5 us (5%)
    all_to_all x1, waiting for transfers between devices, local(): lax.all_to_all(jnp.stack(jnp.split(uncoupled, lax.axis_size('node'), axis...  93.8 us
    div x1, other arithmetic, inverse_factor(): solved_rows.append(running / factor[row_at, row_at])  22.5 us
    dot_general x9, matrix products, mix_planes(): return jnp.einsum('pq,...qb->...pb', matrix, values, precision=precise)  20.3 us
    unnamed x23, local copies, waits for them, and re-layouts  15.8 us
    dot_general x1, matrix products, local(): jnp.einsum('ijpq,sjlqb->lsipb', weights_all, jnp.concatenate(lax.all_to_a...  14.9 us
    psum x1, blocking collectives, local(): pool_sum = lax.psum(jnp.sum(energy, axis=1), 'stripe')  12.1 us
    unnamed x8, other arithmetic  8.71 us
    another operation x1, other arithmetic, local(): fronted = jnp.stack(fronts, axis=1)  6.73 us
  transfers between devices with their start and end apart: 4, of which 2 were waited for; matrix products, arithmetic and copies ran while one was open for 20% of the time, Pallas kernels for 0%

profile of v1, /device:TPU:0, one launch (start us, length us, event | category | flops | bytes accessed | tf_op | source)
XLA Modules:
  0.0 237.1 jit_solution(16338722474759037614)
XLA Ops:
  0.8 2.5 %broadcast_multiply_fusion = bf16[1,2,256,8,512]{4,3,2,1,0:T(8,128)(2,1)S(1)} fusion(bf16[1,2,256,8,512]{4,3,2,1,0:T(8,128)(2,1)} %param.19, bf16[2]{0:T(256)(128)(2,1)S(1)} %or_convert_fusion), kind=kLoop, calls=%fused_computation.61 | loop fusion | flops 2097152 | bytes 8388612 | tf_op jit(solution)/shard_map/mul | solution.py:70
  7.3 3.1 %conditional.4 = (bf16[1,1,4,64,8,512]{5,4,2,3,1,0:T(8,128)(2,1)}) conditional(s32[]{:T(128)} %clamp.8, bf16[1,2,256,8,512]{4,3,2,1,0:T(8,128)(2,1)} %copy-done.6, bf16[1,2,256,8,512]{4,3,2,1,0:T(8,128)(2,1)} %copy-done.6, bf16[1,2,256,8,512]{4,3,2,1,0:T(8,128)(2,1)} %copy-done.6, ...), branch_computations={%region_0.1_spmd, %region_1.2_spmd, %region_2.3_spmd, %region_3.4_... | conditional | bytes 14680096 | solution.py:49
  7.3 3.0 %slice.130 = bf16[1,1,256,8,512]{4,3,2,1,0:T(8,128)(2,1)} slice(bf16[1,2,256,8,512]{4,3,2,1,0:T(8,128)(2,1)} %param), slice={[0:1], [0:1], [0:256], [0:8], [0:512]} | slice | bytes 4194304 | tf_op jit(solution)/shard_map/slice | solution.py:74
  10.3 6.7 %fusion.98 = (bf16[1,2,4,64,8,512]{5,4,3,2,1,0:T(8,128)(2,1)}, f32[1,2,4,64,8,512]{5,4,3,2,1,0:T(8,128)}) fusion(bf16[1,1,4,64,8,512]{5,4,2,3,1,0:T(8,128)(2,1)} %copy-done.7, bf16[1,1,4,64,8,512]{5,4,2,3,1,0:T(8,128)(2,1)} %get-tuple-element.139), kind=kLoop, calls=%fused_computation.140 | loop fusion | flops 4194304 | bytes 16777216 | tf_op jit(solution)/shard_map/stack | solution.py:80
  17.1 3.6 %dynamic-slice_bitcast_fusion = (bf16[1,2,64,8,512]{4,3,2,1,0:T(8,128)(2,1)}, bf16[1,2,64,8,512]{4,3,2,1,0:T(8,128)(2,1)}, bf16[1,2,64,8,512]{4,3,2,1,0:T(8,128)(2,1)}) fusion(bf16[1,2,4,64,8,512]{5,4,3,2,1,0:T(8,128)(2,1)} %get-tuple-element.99, s32[]{:T(128)S(6)} %select_n.139, s32[]{:T(128)S(6)} %select_n.131, s32[]{:T(128)S(6)} %select_n.122), kind=kLoop, calls=%fused_computation.90 | loop fusion | bytes 6291468 | tf_op jit(solution)/shard_map/jit(dynamic_index_in_dim)/squeeze | solution.py:86
  20.6 3.0 %collective-permute-start = (bf16[1,2,64,8,512]{4,3,2,1,0:T(8,128)(2,1)}, bf16[1,2,64,8,512]{4,3,2,1,0:T(8,128)(2,1)S(1)}, u32[]{:S(2)}, u32[]{:S(2)}) collective-permute-start(bf16[1,2,64,8,512]{4,3,2,1,0:T(8,128)(2,1)} %get-tuple-element.98), channel_id=1, source_target_pairs={{24,0},{28,4},{0,8},{4,12},{8,16},{12,20},{16,24},{20,28},{25,1},{... | collective-permute-start | bytes 3145736 | tf_op jit(solution)/shard_map/ppermute | solution.py:22
  28.1 7.6 %copy.163 = f32[1,2,4,64,8,512]{5,4,3,2,1,0:T(8,128)} copy(f32[1,2,4,64,8,512]{5,4,3,2,1,0:T(8,128)} %get-tuple-element.100) | data formatting | bytes 16777216
  38.5 22.5 %subtract_divide_fusion = (f32[1,8]{1,0:T(1,128)S(1)}, f32[1,8]{1,0:T(1,128)S(1)}, f32[1,8]{1,0:T(1,128)S(1)}, f32[1,8]{1,0:T(1,128)S(1)}, f32[1,8]{1,0:T(1,128)...) fusion(f32[8,8]{1,0:T(8,128)S(1)} %fusion.89, f32[]{:T(128)} %bitcast.83, f32[]{:T(128)} %bitcast.82, ...), kind=kLoop, calls=%fused_computation.130 | loop fusion | flops 512 | bytes 656 | tf_op jit(solution)/shard_map/div | solution.py:39
  67.6 2.9 %collective-permute-done.1 = bf16[1,2,64,8,512]{4,3,2,1,0:T(8,128)(2,1)S(1)} collective-permute-done((bf16[1,2,64,8,512]{4,3,2,1,0:T(8,128)(2,1)}, bf16[1,2,64,8,512]{4,3,2,1,0:T(8,128)(2,1)S(1)}, u32[]{:S(2)}, u32[]{:S(2)}) %collective-permute-start.1) | collective-permute-done | bytes 1048608 | tf_op jit(solution)/shard_map/ppermute | solution.py:22
  74.9 2.5 %bitcast_dynamic-update-slice_fusion.2 = f32[1,2,4,64,8,512]{5,4,3,2,1,0:T(8,128)S(1)} fusion(f32[1,2,4,64,8,512]{5,4,3,2,1,0:T(8,128)S(1)} %bitcast.331, s32[]{:T(128)S(6)} %select_n.120, f32[1,2,64,8,512]{4,3,2,1,0:T(8,128)S(1)} %convert_select_fusion.5, f32[2,64,512,8]{2,3,1,0:T(8,128)S(1)} %fusion.4, pred[]{:T(512)S(6)} %lt.82, f32[8,8]{1,0:T(8,128)S(1)} %copy-done), kind=kOutput, calls=%fused_computation.44 | convolution fusion | flops 51380224 | bytes 8392709 | tf_op jit(solution)/shard_map/pq,...qb->...pb/dot_general | solution.py:26
  79.6 2.2 fusion.12
  81.9 2.5 %bitcast_dynamic-update-slice_fusion.1 = f32[1,2,4,64,8,512]{5,4,3,2,1,0:T(8,128)S(1)} fusion(f32[1,2,4,64,8,512]{5,4,3,2,1,0:T(8,128)S(1)} %bitcast_dynamic-update-slice_fusion.2, s32[]{:T(128)S(6)} %select_n.129, f32[2,64,512,8]{2,3,1,0:T(8,128)S(1)} %fusion.8, bf16[1,2,64,8,512]{4,3,2,1,0:T(8,128)(2,1)S(1)} %collective-permute-done.1, ...), kind=kOutput, calls=%fused_computation.38 | convolution fusion | flops 52428800 | bytes 9441285 | tf_op jit(solution)/shard_map/pq,...qb->...pb/dot_general | solution.py:26
  84.3 2.5 %bitcast_dynamic-update-slice_fusion = f32[1,2,4,64,8,512]{5,4,3,2,1,0:T(8,128)S(1)} fusion(f32[1,2,4,64,8,512]{5,4,3,2,1,0:T(8,128)S(1)} %bitcast_dynamic-update-slice_fusion.1, s32[]{:T(128)S(6)} %select_n.137, f32[2,64,512,8]{2,3,1,0:T(8,128)S(1)} %fusion.12, bf16[1,2,64,8,512]{4,3,2,1,0:T(8,128)(2,1)S(1)} %collective-permute-done.2, ...), kind=kOutput, calls=%fused_computation.32 | convolution fusion | flops 52428800 | bytes 9441285 | tf_op jit(solution)/shard_map/pq,...qb->...pb/dot_general | solution.py:26
  86.8 3.2 %copy-done.4 = f32[1,2,4,64,8,512]{5,4,3,2,1,0:T(8,128)} copy-done((f32[1,2,4,64,8,512]{5,4,3,2,1,0:T(8,128)}, f32[1,2,4,64,8,512]{5,4,3,2,1,0:T(8,128)S(1)}, u32[]{:S(2)}) %copy-start.4) | copy-done | bytes 8388632
  90.1 3.3 %conditional.6 = (f32[1,1,256,8,512]{4,3,2,1,0:T(8,128)}) conditional(s32[]{:T(128)} %clamp.8, f32[1,2,4,64,8,512]{5,4,3,2,1,0:T(8,128)S(1)} %bitcast_dynamic-update-slice_fusion, f32[1,2,4,64,8,512]{5,4,3,2,1,0:T(8,128)S(1)} %bitcast_dynamic-update-slice_fusion, ...), branch_computations={%region_10.11_spmd, %region_11.12_spmd, %region_12.13_spmd, %regio... | conditional | bytes 16777224 | solution.py:57
  90.5 2.6 %copy.114 = f32[1,4,4,4,4,8,512]{6,5,1,4,3,2,0:T(8,128)} copy(f32[1,4,4,4,4,8,512]{6,5,4,3,2,1,0:T(8,128)S(1)} %bitcast.335) | data formatting | bytes 8388608 | tf_op jit(solution)/shard_map/reshape;squeeze | solution.py:106
  93.3 5.1 %conditional.7 = (f32[1,1,256,8,512]{4,3,2,1,0:T(8,128)}) conditional(s32[]{:T(128)} %clamp.9, f32[1,2,4,64,8,512]{5,4,3,2,1,0:T(8,128)} %copy-done.4, f32[1,2,4,64,8,512]{5,4,3,2,1,0:T(8,128)} %copy-done.4, f32[1,2,4,64,8,512]{5,4,3,2,1,0:T(8,128)} %copy-done.4, f32[1,2,4,64,8,512]{5,4,3,2,1,0:T(8,128)} %copy-done.4), branch_computations={%region_14.15_spmd, %region_15.16_spmd, %region_16.17_spmd, %regio... | conditional | bytes 16777224 | solution.py:57
  93.4 2.6 %slice.143 = f32[1,1,4,64,8,512]{5,4,3,2,1,0:T(8,128)S(1)} slice(f32[1,2,4,64,8,512]{5,4,3,2,1,0:T(8,128)} %param.13), slice={[0:1], [1:2], [0:4], [0:64], [0:8], [0:512]} | slice | bytes 8388608 | tf_op jit(solution)/shard_map/slice | solution.py:106
  96.0 2.4 %copy.118 = f32[1,4,4,4,4,8,512]{6,5,4,1,3,2,0:T(8,128)} copy(f32[1,4,4,4,4,8,512]{6,5,4,3,2,1,0:T(8,128)S(1)} %bitcast.339) | data formatting | bytes 8388608 | tf_op jit(solution)/shard_map/reshape;squeeze | solution.py:106
  98.4 2.4 %fusion.44 = f32[8,1,2,32,8,512]{5,4,3,2,1,0:T(8,128)} fusion(f32[1,1,256,8,512]{4,3,2,1,0:T(8,128)} %get-tuple-element.141, f32[1,1,256,8,512]{4,3,2,1,0:T(8,128)} %get-tuple-element.142), kind=kLoop, calls=%fused_computation.71 | loop fusion | flops 262143 | bytes 9437184
  110.0 5.2 %all-to-all-start = ((f32[8,1,2,32,8,512]{5,4,3,2,1,0:T(8,128)}), f32[8,1,2,32,8,512]{5,4,3,2,1,0:T(8,128)}, u32[]{:S(2)}, u32[]{:S(2)}) async-start(f32[8,1,2,32,8,512]{5,4,3,2,1,0:T(8,128)} %fusion.61), calls=%async_computation | async-start | bytes 16777216 | tf_op jit(solution)/shard_map/all_to_all | solution.py:118
  115.4 93.8 %all-to-all-done = f32[8,1,2,32,8,512]{5,4,3,2,1,0:T(8,128)} async-done(((f32[8,1,2,32,8,512]{5,4,3,2,1,0:T(8,128)}), f32[8,1,2,32,8,512]{5,4,3,2,1,0:T(8,128)}, u32[]{:S(2)}, u32[]{:S(2)}) %all-to-all-start) | async-done | bytes 8388640 | tf_op jit(solution)/shard_map/all_to_all | solution.py:118
  209.2 14.9 %fusion.26 = (f32[32,4]{1,0:T(8,128)S(1)}, f32[32,512,4,8,1]{1,3,4,2,0:T(8,128)}) fusion(f32[4,4,8,8]{1,2,3,0:T(8,128)S(1)} %broadcast_multiply_fusion.1, f32[4,12,8,8]{1,2,3,0:T(8,128)S(1)} %copy_negate_fusion, f32[16,32,8,512,1]{3,2,1,0,4:T(8,128)} %bitcast.134), kind=kOutput, calls=%fused_computation.51 | convolution fusion | flops 806358912 | bytes 10502656 | tf_op jit(solution)/shard_map/ijpq,sjlqb->lsipb/dot_general | solution.py:114
  224.2 12.1 %psum.7 = f32[32,4]{0,1:T(4,128)S(1)} all-reduce(f32[32,4]{0,1:T(4,128)S(1)} %broadcast_multiply_fusion.2), channel_id=1, replica_groups=mesh['node'=8,'stripe'=4] {'stripe'}, use_global_device_ids=true, to_apply=%region_19.20 | all-reduce | flops 128 | bytes 1024 | tf_op jit(solution)/shard_map/psum | solution.py:126
  (64 shorter events, 35.3 us)
Async XLA Ops:
  0.6 26.4 %copy-start = (f32[8,8]{1,0:T(8,128)S(1)}, f32[8,8]{1,0:T(8,128)}, u32[]{:S(2)}) copy-start(f32[8,8]{1,0:T(8,128)} %param.20) | copy-start | bytes 772
  3.3 1.9 copy-start.6
  5.9 1.3 copy-start.7
  20.6 40.6 %collective-permute-start = (bf16[1,2,64,8,512]{4,3,2,1,0:T(8,128)(2,1)}, bf16[1,2,64,8,512]{4,3,2,1,0:T(8,128)(2,1)S(1)}, u32[]{:S(2)}, u32[]{:S(2)}) collective-permute-start(bf16[1,2,64,8,512]{4,3,2,1,0:T(8,128)(2,1)} %get-tuple-element.98), channel_id=1, source_target_pairs={{24,0},{28,4},{0,8},{4,12},{8,16},{12,20},{16,24},{20,28},{25,1},{... | collective-permute-start | bytes 3145736 | tf_op jit(solution)/shard_map/ppermute | solution.py:22
  23.6 47.0 %collective-permute-start.1 = (bf16[1,2,64,8,512]{4,3,2,1,0:T(8,128)(2,1)}, bf16[1,2,64,8,512]{4,3,2,1,0:T(8,128)(2,1)S(1)}, u32[]{:S(2)}, u32[]{:S(2)}) collective-permute-start(bf16[1,2,64,8,512]{4,3,2,1,0:T(8,128)(2,1)} %get-tuple-element.97), channel_id=1, source_target_pairs={{16,0},{20,4},{24,8},{28,12},{0,16},{4,20},{8,24},{12,28},{17,1},{... | collective-permute-start | bytes 3145736 | tf_op jit(solution)/shard_map/ppermute | solution.py:22
  25.1 52.4 %collective-permute-start.2 = (bf16[1,2,64,8,512]{4,3,2,1,0:T(8,128)(2,1)}, bf16[1,2,64,8,512]{4,3,2,1,0:T(8,128)(2,1)S(1)}, u32[]{:S(2)}, u32[]{:S(2)}) collective-permute-start(bf16[1,2,64,8,512]{4,3,2,1,0:T(8,128)(2,1)} %get-tuple-element.96), channel_id=1, source_target_pairs={{8,0},{12,4},{16,8},{20,12},{24,16},{28,20},{0,24},{4,28},{9,1},{1... | collective-permute-start | bytes 3145736 | tf_op jit(solution)/shard_map/ppermute | solution.py:22
  61.3 4.1 %copy-start.5 = (f32[1,2,4,64,8,512]{5,4,3,2,1,0:T(8,128)S(1)}, f32[1,2,4,64,8,512]{5,4,3,2,1,0:T(8,128)}, u32[]{:S(2)}) copy-start(f32[1,2,4,64,8,512]{5,4,3,2,1,0:T(8,128)} %get-tuple-element.100) | copy-start | bytes 25165828
  65.4 9.5 %slice-start = ((s8[8388608]{0:T(1024)(128)(4,1)}), s8[4194304]{0:T(1024)(128)(4,1)S(1)}, s32[]{:S(2)}) async-start(s8[8388608]{0:T(1024)(128)(4,1)} %bitcast.330), calls=%async_computation.1 | async-start | bytes 8388608
  67.6 7.3 %slice-start.1 = ((s8[8388608]{0:T(1024)(128)(4,1)}), s8[4194304]{0:T(1024)(128)(4,1)S(1)}, s32[]{:S(2)}) async-start(s8[8388608]{0:T(1024)(128)(4,1)} %bitcast.330), calls=%async_computation.2 | async-start | bytes 8388608
  86.8 3.3 %copy-start.4 = (f32[1,2,4,64,8,512]{5,4,3,2,1,0:T(8,128)}, f32[1,2,4,64,8,512]{5,4,3,2,1,0:T(8,128)S(1)}, u32[]{:S(2)}) copy-start(f32[1,2,4,64,8,512]{5,4,3,2,1,0:T(8,128)S(1)} %bitcast_dynamic-update-slice_fusion) | copy-start | bytes 25165828
  98.4 2.9 %copy-start.2 = (f32[1,1,256,8,512]{4,3,2,1,0:T(8,128)S(1)}, f32[1,1,256,8,512]{4,3,2,1,0:T(8,128)}, u32[]{:S(2)}) copy-start(f32[1,1,256,8,512]{4,3,2,1,0:T(8,128)} %get-tuple-element.141) | copy-start | bytes 12582916
  98.4 4.2 %copy-start.3 = (f32[1,1,256,8,512]{4,3,2,1,0:T(8,128)S(1)}, f32[1,1,256,8,512]{4,3,2,1,0:T(8,128)}, u32[]{:S(2)}) copy-start(f32[1,1,256,8,512]{4,3,2,1,0:T(8,128)} %get-tuple-element.142) | copy-start | bytes 12582916
  110.0 5.3 %copy-start.8 = (f32[4,12,8,8]{1,3,2,0:T(8,128)S(1)}, f32[4,12,8,8]{1,3,2,0:T(8,128)}, u32[]{:S(2)}) copy-start(f32[4,12,8,8]{1,3,2,0:T(8,128)} %param.21) | copy-start | bytes 36868
  110.0 99.2 %all-to-all-start = ((f32[8,1,2,32,8,512]{5,4,3,2,1,0:T(8,128)}), f32[8,1,2,32,8,512]{5,4,3,2,1,0:T(8,128)}, u32[]{:S(2)}, u32[]{:S(2)}) async-start(f32[8,1,2,32,8,512]{5,4,3,2,1,0:T(8,128)} %fusion.61), calls=%async_computation | async-start | bytes 16777216 | tf_op jit(solution)/shard_map/all_to_all | solution.py:118
  209.2 27.7 %copy-start.1 = (f32[8,8]{1,0:T(8,128)S(1)}, f32[8,8]{1,0:T(8,128)}, u32[]{:S(2)}) copy-start(f32[8,8]{1,0:T(8,128)} %param.20) | copy-start | bytes 772
